TPU v7x, 16 devices: a 4x2x1 block of a 4x4x8 slice. The times are simulated.
16 devices in a mesh: dp: 2 (over y, z), tp: 8 (over x, core).
Axes of the slice: x: 4, y: 2, z: 1, core: 2. Of those that a mesh axis runs over, the one named last changes fastest.
The devices are a block of a 4x4x8 slice.
Arguments:
- token_ids: int32 [16384], P('dp'), parts along dimension 0
- embed_table: bfloat16 [151936, 896], P('tp')
- norm_gain: bfloat16 [896], replicated
- w_in: bfloat16 [896, 4864], P(None, 'tp')
- w_out: bfloat16 [4864, 896], P('tp')
Outputs:
- output: bfloat16 [16384, 896], P(('dp', 'tp')), parts along dimension 0
There are 2 independent parts. A program takes and returns all parts, laid end to end along the dimension named above; an argument that names none is the same for every part.
All inputs are finite; a program needn't handle non-finite values.
Results may differ from a plain program's by a relative error of at most 0.0079017.
Values are sent between devices in bfloat16 or wider.
A program may use at most 768 MiB of HBM per device.

v0:
```python
import functools

import jax
import jax.numpy as jnp
from jax import lax
from jax.experimental import pallas as pl
from jax.experimental.pallas import tpu as pltpu
from jax.sharding import PartitionSpec as P

RMS_EPS = 1e-6
MESH = pl.DeviceIdType.MESH
SUB = 8
GELU_C = 0.7978845608028654
N_COPIES = 40


def gelu(u):
    z = u.astype(jnp.bfloat16).astype(jnp.float32)
    h = 0.5 * z * (1.0 + jnp.tanh(GELU_C * (z + 0.044715 * (z * z * z))))
    return h.astype(jnp.bfloat16)


def pick_rows(rows, idx_ref, base):
    width = rows.shape[-1]
    iota = lax.broadcasted_iota(jnp.int32, (SUB, width), 0)
    acc = None
    for p in range(SUB):
        code = idx_ref[base + p]
        at = jnp.minimum(jnp.maximum(lax.shift_right_logical(code, 3), 0), rows.shape[0] - 1)
        tile = rows[at].astype(jnp.float32)
        tile = pltpu.roll(tile, (code + p) & 7, 0)
        acc = tile if acc is None else jnp.where(iota == p, tile, acc)
    return acc


def pick_16(rows, idx_ref, base):
    parts = [pick_rows(rows, idx_ref, base), pick_rows(rows, idx_ref, base + SUB)]
    return jnp.concatenate(parts, axis=0).astype(jnp.bfloat16)


def slot_tables(ids_ref, keys, slots_v, over_ref, chip, tp, chips, shard_rows, cap):
    f32 = jnp.float32
    lines = ids_ref.shape[0]
    dests = 2 * chips
    per = lines // dests
    ids = ids_ref[...]
    span = 2 * shard_rows
    lane = lax.broadcasted_iota(jnp.int32, (lines, 128), 1)
    row = lax.broadcasted_iota(jnp.int32, (lines, 128), 0) & (per - 1)
    top = None
    for s in range(chips):
        mask = (ids >= s * span) & (ids < (s + 1) * span)
        upto = jnp.where(mask, 1, 0)
        for k in range(7):
            upto = upto + jnp.where(lane >= 2**k, pltpu.roll(upto, 2**k, 1), 0)
        sums = jnp.where(lane == 127, upto, 0)
        for k in range(7):
            sums = sums + pltpu.roll(sums, 2**k, 1)
        before = jnp.where(row >= 1, pltpu.roll(sums, 1, 0), 0)
        for k in range(per.bit_length() - 1):
            before = before + jnp.where(row >= 2**k, pltpu.roll(before, 2**k, 0), 0)
        key = jnp.where(mask, upto + before - 1, -1)
        keys[pl.ds(s * lines, lines), :] = key
        key = key.astype(f32)
        top = key if top is None else jnp.maximum(top, key)
    over_ref[...] = jnp.zeros(over_ref.shape, f32) + jnp.max(top, axis=(0, 1), keepdims=True)

    lanes = slots_v.shape[1]
    slot_id = lax.broadcasted_iota(jnp.int32, (128, lanes), 1)
    first = tp * shard_rows
    none = shard_rows

    def one_dest(d, carry):
        at = pl.ds(pl.multiple_of(d * per, per), per)
        local = ids_ref[at, :] - first
        here = (local >= 0) & (local < shard_rows)
        k = keys[pl.ds(pl.multiple_of(chip * lines + d * per, per), per), :]
        key_t = jnp.transpose(jnp.where(here, k, -1))
        code = (local - (local & 7)) + ((SUB - (local & 7)) & 7)
        row_t = jnp.transpose(code - none)
        acc = jnp.zeros((128, lanes), jnp.int32)
        for r in range(per):
            acc = acc + jnp.where(key_t[:, r : r + 1] == slot_id, row_t[:, r : r + 1], 0)
        slots_v[pl.ds(d, 1), :] = jnp.clip(jnp.sum(acc, axis=0, keepdims=True) + none, 0, none)
        return carry

    lax.fori_loop(0, dests, one_dest, 0)


def block_kernel(chips, ids_ref, table_hbm, gain_ref, w1_hbm, w2_hbm, out_hbm, over_ref, w1_all, w2_all,
                 table, own, sib_part, for_sib, got, fwd_up, fwd_dn, y_ref, w_buf, keys, slots_v, sidx,
                 tab_sem, loc_sem, ss, rs):
    dp, tp = lax.axis_index("dp"), lax.axis_index("tp")
    chip, core = tp // 2, lax.rem(tp, 2)
    half = lax.rem(dp, 2)
    other = 1 - core
    sib = {"tp": chip * 2 + other}
    up = {"tp": lax.rem(chip + 1, chips) * 2 + core}
    dn = {"tp": lax.rem(chip + chips - 1, chips) * 2 + core}
    pair = {"dp": dp + 1 - 2 * half}
    cap = own.shape[0] // 3
    mid = cap // 2
    hid, width = w1_hbm.shape
    tokens = out_hbm.shape[0]
    counter = iter(range(N_COPIES))

    def rcopy(src, dst, dev):
        n = next(counter)
        return pltpu.make_async_remote_copy(src_ref=src, dst_ref=dst, send_sem=ss.at[n], recv_sem=rs.at[n],
                                            device_id=dev, device_id_type=MESH)

    n_tab = tab_sem.shape[0]
    tab_copies = []
    tiles = table.shape[0] - 1
    for i in range(n_tab):
        lo, hi = tiles * i // n_tab, tiles * (i + 1) // n_tab
        tab_copies.append(pltpu.make_async_copy(table_hbm.at[pl.ds(lo, hi - lo)], table.at[pl.ds(lo, hi - lo)],
                                                tab_sem.at[i]))

    barrier = pltpu.get_barrier_semaphore()
    for dev in (sib, up, dn, pair):
        pl.semaphore_signal(barrier, inc=1, device_id=dev, device_id_type=MESH)
    for copy in tab_copies:
        copy.start()
    pl.semaphore_wait(barrier, 4)

    hh = hid // 2

    def wrow(j, c, h=None):
        start = (j * 2 + c) * hid
        if h is None:
            return pl.ds(pl.multiple_of(start, 16), hid)
        return pl.ds(pl.multiple_of(start + h * hh, 16), hh)

    hrow = pl.ds(pl.multiple_of(half * hh, 16), hh)
    w_in = {1: w1_hbm, 2: w2_hbm}
    w_all = {1: w1_all, 2: w2_all}

    wx, wy, wd = {}, {}, {}
    for m in (1, 2):
        wx[1, m] = rcopy(w_in[m].at[hrow], w_all[m].at[wrow(1, core, half)], up)
        wx[3, m] = rcopy(w_in[m].at[hrow], w_all[m].at[wrow(3, core, half)], dn)
    split = hid * 9 // 38 // 16 * 16
    common = hid - 2 * split

    def far(j, part):
        if part == 0:
            return pl.ds(pl.multiple_of((j * 2 + core) * hid, 16), common)
        which = half if part == 1 else 1 - half
        return pl.ds(pl.multiple_of((j * 2 + core) * hid + common + which * split, 16), split)

    for part in (1, 0):
        wx[2, 1, part] = rcopy(w1_all.at[far(1, part)], w1_all.at[far(2, part)], up)
        wx[2, 2, part] = rcopy(w2_all.at[far(3, part)], w2_all.at[far(2, part)], dn)
    for m in (1, 2):
        wy[2, m] = rcopy(w_all[m].at[far(2, 1)], w_all[m].at[far(2, 1)], pair)
        for part in (0, 1, 2):
            wd[2, m, part] = rcopy(w_all[m].at[far(2, part)], w_all[m].at[far(2, part)], sib)
    for m in (1, 2):
        for j in (1, 3):
            wy[j, m] = rcopy(w_all[m].at[wrow(j, core, half)], w_all[m].at[wrow(j, core, half)], pair)
        wd[0, m] = rcopy(w_in[m], w_all[m].at[wrow(0, core)], sib)
        for j in (1, 3):
            for k, h in ((0, half), (1, 1 - half)):
                wd[j, m, k] = rcopy(w_all[m].at[wrow(j, core, h)], w_all[m].at[wrow(j, core, h)], sib)

    d2d = {}
    for n, j in enumerate((2, 1, 3, 0)):
        d2d[j] = rcopy(for_sib.at[pl.ds((n % 2) * cap, cap)], sib_part.at[pl.ds(j * cap, cap)], sib)
    rows = {
        "2u": rcopy(own.at[pl.ds(cap, mid)], fwd_up, up),
        "2d": rcopy(own.at[pl.ds(cap + mid, mid)], fwd_dn, dn),
        1: rcopy(own.at[pl.ds(0, cap)], got.at[pl.ds(cap, cap)], up),
        3: rcopy(own.at[pl.ds(2 * cap, cap)], got.at[pl.ds(3 * cap, cap)], dn),
        "fu": rcopy(fwd_up, got.at[pl.ds(2 * cap, mid)], up),
        "fd": rcopy(fwd_dn, got.at[pl.ds(2 * cap + mid, mid)], dn),
    }

    for key in ((1, 1), (3, 1), (1, 2), (3, 2)):
        wx[key].start()
    wd[0, 1].start()
    wd[0, 2].start()
    slot_tables(ids_ref, keys, slots_v, over_ref, chip, tp, chips, tiles * SUB, cap)
    table[tiles] = jnp.zeros((SUB, width), jnp.bfloat16)
    lanes = slots_v.shape[1]
    fetch = [
        pltpu.make_async_copy(slots_v.at[d], sidx.at[pl.ds(d * lanes, lanes)], loc_sem.at[4 * chips + 2 + d])
        for d in range(2 * chips)
    ]
    for copy in fetch:
        copy.start()
    for copy in fetch:
        copy.wait()
    for copy in tab_copies:
        copy.wait()

    def pick_slots(j, c, dst, at):
        base = (lax.rem(chip + j, chips) * 2 + c) * lanes

        def body(i, carry):
            dst[pl.ds(pl.multiple_of(at + i * 16, 16), 16), :] = pick_16(table, sidx, base + i * 16)
            return carry

        lax.fori_loop(0, cap // 16, body, 0)

    def add_part(j):
        d2d[j].wait_recv()
        ref, at = (got, 0) if j == 0 else (own, (j - 1) * cap)

        def body(i, carry):
            a = pl.ds(pl.multiple_of(at + i * 32, 32), 32)
            ref[a, :] = ref[a, :] + sib_part[pl.ds(pl.multiple_of(j * cap + i * 32, 32), 32), :]
            return carry

        lax.fori_loop(0, cap // 32, body, 0)

    def pick_sib(n, j):
        pick_slots(j, other, for_sib, (n % 2) * cap)
        d2d[j].start()

    def pick_own(j):
        if j == 0:
            pick_slots(j, core, got, 0)
        else:
            pick_slots(j, core, own, (j - 1) * cap)

    pick_sib(0, 2)
    pick_own(2)
    pick_sib(1, 1)
    add_part(2)
    rows["2u"].start()
    rows["2d"].start()
    pick_own(1)
    d2d[2].wait_send()
    pick_sib(2, 3)
    add_part(1)
    rows[1].start()
    for j in (1, 3):
        wx[j, 1].wait_recv()
        wy[j, 1].start()
    pick_own(3)
    add_part(3)
    rows[3].start()
    for j in (1, 3):
        wx[j, 2].wait_recv()
        wy[j, 2].start()
    d2d[1].wait_send()
    pick_sib(3, 0)
    pick_own(0)
    add_part(0)

    slot = {0: 0, 1: 1, 3: 0, 2: 1}
    piece = 2 * hid
    load = {}
    for j in range(chips):
        for m in (1, 2):
            base = (slot[j] * 2 + m - 1) * piece
            n = (j * 2 + m - 1) * 2
            if j == 0:
                load[j, m] = [
                    pltpu.make_async_copy(w_in[m], w_buf.at[pl.ds(pl.multiple_of(base + core * hid, 16), hid)],
                                          loc_sem.at[n]),
                    pltpu.make_async_copy(w_all[m].at[wrow(0, other)],
                                          w_buf.at[pl.ds(pl.multiple_of(base + other * hid, 16), hid)],
                                          loc_sem.at[n + 1]),
                ]
            else:
                load[j, m] = [
                    pltpu.make_async_copy(w_all[m].at[pl.ds(j * piece, piece)], w_buf.at[pl.ds(base, piece)],
                                          loc_sem.at[n])
                ]

    def start_load(j):
        for m in (1, 2):
            for copy in load[j, m]:
                copy.start()

    for m in (1, 2):
        wd[0, m].wait_recv()
    start_load(0)
    rows["2u"].wait_recv()
    rows["fu"].start()
    rows["2d"].wait_recv()
    rows["fd"].start()
    for j in (1, 3):
        for m in (1, 2):
            wd[j, m, 0].start()
    for m in (1, 2):
        for j in (1, 3):
            wy[j, m].wait_recv()
            wd[j, m, 1].start()
            if (j, m) == (1, 1) or (j, m) == (3, 2):
                wx[2, m, 1].start()
                wx[2, m, 0].start()

    gain = gain_ref[...].astype(jnp.float32)
    lines = tokens // 128
    slot_id = lax.broadcasted_iota(jnp.int32, (128, cap), 1).astype(jnp.float32)

    def place(sources, start, finish):
        def body(i, carry):
            at = pl.ds(pl.multiple_of(i * 512, 512), 512)
            total = None if start else y_ref[at, :]
            for j in sources:
                line = lax.rem(chip + chips - j, chips) * ids_ref.shape[0] + tp * lines
                key_t = jnp.transpose(keys[pl.ds(pl.multiple_of(line, SUB), SUB), :].astype(jnp.float32))
                lane = lax.broadcasted_iota(jnp.int32, key_t.shape, 1)
                hits = []
                for r in range(4):
                    col = jnp.sum(jnp.where(lane == 4 * i + r, key_t, 0.0), axis=1, keepdims=True)
                    hits.append(jnp.where(col == slot_id, 1.0, 0.0).astype(jnp.bfloat16))
                part = jnp.dot(jnp.concatenate(hits, axis=0), got[pl.ds(j * cap, cap), :],
                               preferred_element_type=jnp.float32)
                total = part if total is None else total + part
            if not finish:
                y_ref[at, :] = total
                return carry
            inv = lax.rsqrt(jnp.mean(total * total, axis=-1, keepdims=True) + RMS_EPS)
            sib_part[at, :] = total.astype(jnp.bfloat16)
            sib_part[pl.ds(pl.multiple_of(tokens + i * 512, 512), 512), :] = (total * inv * gain).astype(jnp.bfloat16)
            return carry

        lax.fori_loop(0, tokens // 512, body, 0)

    place((0,), True, False)
    rows[1].wait_recv()
    rows[3].wait_recv()
    place((1, 3), False, False)
    rows["fu"].wait_recv()
    rows["fd"].wait_recv()
    place((2,), False, True)

    block = 512

    def mlp(j, first=False, last=False):
        for m in (1, 2):
            for copy in load[j, m]:
                copy.wait()
        base = slot[j] * 2 * piece

        def body(i, carry):
            at = pl.ds(pl.multiple_of(i * block, block), block)
            n = sib_part[pl.ds(pl.multiple_of(tokens + i * block, block), block), :]
            u = lax.dot_general(n, w_buf[pl.ds(base, piece), :], (((1,), (1,)), ((), ())),
                                preferred_element_type=jnp.float32)
            y = jnp.dot(gelu(u), w_buf[pl.ds(base + piece, piece), :], preferred_element_type=jnp.float32)
            if not first:
                y = y_ref[at, :] + y
            if last:
                sib_part[at, :] = (sib_part[at, :].astype(jnp.float32) + y).astype(jnp.bfloat16)
            else:
                y_ref[at, :] = y
            return carry

        lax.fori_loop(0, tokens // block, body, 0)

    def arrived(j):
        for m in (1, 2):
            for k in (0, 1, 2) if j == 2 else (0, 1):
                wd[j, m, k].wait_recv()
        start_load(j)

    arrived(1)
    mlp(0, first=True)
    arrived(3)
    mlp(1)
    for m in (1, 2):
        wx[2, m, 1].wait_recv()
        wy[2, m].start()
        wd[2, m, 1].start()
    mlp(3)
    for m in (1, 2):
        wx[2, m, 0].wait_recv()
        wd[2, m, 0].start()
    for m in (1, 2):
        wy[2, m].wait_recv()
        wd[2, m, 2].start()
    arrived(2)
    mlp(2, last=True)
    store = pltpu.make_async_copy(sib_part.at[pl.ds(0, tokens)], out_hbm, loc_sem.at[4 * chips + 1])
    store.start()
    store.wait()

    d2d[3].wait_send()
    d2d[0].wait_send()
    for group in (wx, wy, wd, rows):
        for copy in group.values():
            copy.wait_send()


def copy_kernel(src, dst):
    dst[...] = src[...]


def settle(res):
    rows, width = res.shape
    spec = pl.BlockSpec((rows // 4, width), lambda i: (i, 0))
    return pl.pallas_call(
        copy_kernel,
        out_shape=jax.ShapeDtypeStruct(res.shape, res.dtype),
        grid=(4,),
        in_specs=[spec],
        out_specs=spec,
    )(res)


def solution(mesh):
    ranks = mesh.shape["tp"]
    chips = ranks // 2

    def device_step(token_ids, table, norm_gain, w1, w2):
        shard_rows, width = table.shape
        tokens = token_ids.shape[0] // ranks
        tp = lax.axis_index("tp")
        cap = tokens * 17 // 32
        hidden = w1.shape[1]
        bf, f32 = jnp.bfloat16, jnp.float32
        dma = pltpu.SemaphoreType.DMA
        anyspec = pl.BlockSpec(memory_space=pl.ANY)
        vmem = pl.BlockSpec(memory_space=pltpu.VMEM)
        lines = token_ids.shape[0] // 128
        lanes = -(-cap // 128) * 128
        out, top, w1_all, w2_all = pl.pallas_call(
            functools.partial(block_kernel, chips),
            out_shape=[
                jax.ShapeDtypeStruct((tokens, width), bf),
                jax.ShapeDtypeStruct((SUB, 128), f32),
                jax.ShapeDtypeStruct((ranks * hidden, width), bf),
                jax.ShapeDtypeStruct((ranks * hidden, width), bf),
            ],
            in_specs=[vmem, anyspec, vmem, anyspec, anyspec],
            out_specs=[anyspec, vmem, anyspec, anyspec],
            scratch_shapes=[
                pltpu.VMEM((shard_rows // SUB + 1, SUB, width), bf),
                pltpu.VMEM((3 * cap, width), bf),
                pltpu.VMEM((4 * cap, width), bf),
                pltpu.VMEM((2 * cap, width), bf),
                pltpu.VMEM((4 * cap, width), bf),
                pltpu.VMEM((cap // 2, width), bf),
                pltpu.VMEM((cap // 2, width), bf),
                pltpu.VMEM((tokens, width), f32),
                pltpu.VMEM((8 * hidden, width), bf),
                pltpu.VMEM((chips * lines, 128), jnp.int32),
                pltpu.VMEM((ranks, lanes), jnp.int32),
                pltpu.SMEM((ranks * lanes,), jnp.int32),
                dma((8,)), dma((4 * chips + 2 + ranks,)),
                dma((N_COPIES,)), dma((N_COPIES,)),
            ],
            compiler_params=pltpu.CompilerParams(
                collective_id=0, has_side_effects=True, vmem_limit_bytes=67043328
            ),
        )(token_ids.reshape(lines, 128), table.reshape(shard_rows // SUB, SUB, width), norm_gain.reshape(1, width), w1.T, w2)
        overflow = top[0, 0] >= cap

        def plain(_):
            local = token_ids - tp * shard_rows
            owned = (local >= 0) & (local < shard_rows)
            found = jnp.take(table, jnp.clip(local, 0, shard_rows - 1), axis=0, mode="clip")
            part = jnp.where(owned[:, None], found, jnp.zeros((), bf)).reshape(ranks, tokens, width)
            x = jnp.sum(lax.all_to_all(part, "tp", 0, 0).astype(f32), axis=0)
            w1s = lax.dynamic_update_slice(w1_all, w1.T, ((tp % 2) * hidden, 0))
            w2s = lax.dynamic_update_slice(w2_all, w2, ((tp % 2) * hidden, 0))
            inv = lax.rsqrt(jnp.mean(x * x, axis=-1, keepdims=True) + RMS_EPS)
            n = (x * inv * norm_gain.astype(f32)).astype(bf)
            u = lax.dot_general(n, w1s, (((1,), (1,)), ((), ())), preferred_element_type=f32)
            y = jnp.dot(gelu(u), w2s, preferred_element_type=f32)
            return (x + y).astype(bf)

        return lax.cond(overflow, plain, settle, out)

    return jax.shard_map(
        device_step,
        mesh=mesh,
        in_specs=(P("dp"), P("tp", None), P(), P(None, "tp"), P("tp", None)),
        out_specs=P(("dp", "tp"), None),
        check_vma=False,
    )
```

profile of v0, /device:TPU:112, one launch (start us, length us, event | category | flops | bytes accessed | tf_op | source)
XLA Modules:
  0.0 123.1 jit_solution(17158810750553363720)
XLA Ops:
  0.0 1.3 %reshape.32.gain_ref = bf16[1,896]{1,0:T(2,128)(2,1)} reshape(bf16[896]{0:T(1024)(128)(2,1)} %param.9) | data formatting | bytes 3584 | tf_op jit(solution)/shard_map/reshape | solution.py:452
  1.3 116.4 %shard_map.57 = (bf16[1024,896]{1,0:T(8,128)(2,1)}, f32[8,128]{1,0:T(8,128)}, bf16[4864,896]{1,0:T(8,128)(2,1)}, bf16[4864,896]{1,0:T(8,128)(2,1)}) custom-call(s32[64,128]{1,0:T(8,128)} %bitcast.12, bf16[2374,8,896]{2,1,0:T(8,128)(2,1)} %bitcast.8, bf16[1,896]{1,0:T(2,128)(2,1)} %reshape.32.gain_ref, bf16[608,896]{1,0:T(8,128)(2,1)} %bitcast.11, ...), custom_call_target="tpu_custom_call" | custom-call | tf_op jit(solution)/shard_map/pallas_call | solution.py:423
  117.7 1.2 slice.3
  119.5 2.3 %conditional.1 = (bf16[1024,896]{1,0:T(8,128)(2,1)S(1)}) conditional(s32[]{:T(128)} %bitcast.5, bf16[1024,896]{1,0:T(8,128)(2,1)} %get-tuple-element.38, (s32[]{:T(128)}, s32[8192]{0:T(1024)}, bf16[18992,896]{1,0:T(8,128)(2,1)}, bf16[896]{0:T(1024)(128)(2,1)}, bf16[896,608]{0,1:T(8,128)(2,1)}, /*index=5*/bf16[4864,896]{1,0:T(8,128)(2,1)}, ...), branch_computations={%region_0.0_spmd, %region_1.4_spmd} | conditional | flops 17933330432 | bytes 195280992 | solution.py:469
  119.5 2.3 %branch_0_fun.1 = bf16[1024,896]{1,0:T(8,128)(2,1)S(1)} custom-call(bf16[1024,896]{1,0:T(8,128)(2,1)} %src), custom_call_target="tpu_custom_call" | custom-call | tf_op jit(solution)/shard_map/cond/branch_0_fun/pallas_call | solution.py:398
  121.8 0.0 copy-start.3
  121.9 1.2 copy-done.3
Async XLA Ops:
  121.8 1.2 %copy-start.3 = (bf16[1024,896]{1,0:T(8,128)(2,1)}, bf16[1024,896]{1,0:T(8,128)(2,1)S(1)}, u32[]{:S(2)}) copy-start(bf16[1024,896]{1,0:T(8,128)(2,1)S(1)} %get-tuple-element.54) | copy-start | bytes 5505028
where the time goes:
time: 125 us; the launch traced here: 123 us
  Pallas kernels  119 us (95%)
  local copies, waits for them, and re-layouts  3.68 us (3%)
    pallas_call x1, Pallas kernels, device_step(): pl.pallas_call(functools.partial(block_kernel, chips), out_shape=[jax.Sha...  116 us

commit v1 on v0

--- a/solution.py
+++ b/solution.py
@@ -11,7 +11,7 @@
 MESH = pl.DeviceIdType.MESH
 SUB = 8
 GELU_C = 0.7978845608028654
-N_COPIES = 40
+N_COPIES = 52
 
 
 def gelu(u):
@@ -38,7 +38,11 @@
     return jnp.concatenate(parts, axis=0).astype(jnp.bfloat16)
 
 
-def slot_tables(ids_ref, keys, slots_v, over_ref, chip, tp, chips, shard_rows, cap):
+def slot_split(tokens):
+    return tokens * 15 // 64, tokens * 9 // 32
+
+
+def slot_tables(ids_ref, keys, slots_v, over_ref, chip, tp, chips, shard_rows, base):
     f32 = jnp.float32
     lines = ids_ref.shape[0]
     dests = 2 * chips
@@ -47,9 +51,8 @@
     span = 2 * shard_rows
     lane = lax.broadcasted_iota(jnp.int32, (lines, 128), 1)
     row = lax.broadcasted_iota(jnp.int32, (lines, 128), 0) & (per - 1)
-    top = None
-    for s in range(chips):
-        mask = (ids >= s * span) & (ids < (s + 1) * span)
+
+    def scan(mask):
         upto = jnp.where(mask, 1, 0)
         for k in range(7):
             upto = upto + jnp.where(lane >= 2**k, pltpu.roll(upto, 2**k, 1), 0)
@@ -59,7 +62,19 @@
         before = jnp.where(row >= 1, pltpu.roll(sums, 1, 0), 0)
         for k in range(per.bit_length() - 1):
             before = before + jnp.where(row >= 2**k, pltpu.roll(before, 2**k, 0), 0)
-        key = jnp.where(mask, upto + before - 1, -1)
+        return upto + before - 1
+
+    ranks = []
+    extra = None
+    for s in range(chips):
+        mask = (ids >= s * span) & (ids < (s + 1) * span)
+        rank = jnp.where(mask, scan(mask), -1)
+        ranks.append(rank)
+        extra = rank if extra is None else jnp.maximum(extra, rank)
+    shared = scan(extra >= base) + base
+    top = None
+    for s in range(chips):
+        key = jnp.where(ranks[s] >= base, shared, ranks[s])
         keys[pl.ds(s * lines, lines), :] = key
         key = key.astype(f32)
         top = key if top is None else jnp.maximum(top, key)
@@ -99,9 +114,12 @@
     dn = {"tp": lax.rem(chip + chips - 1, chips) * 2 + core}
     pair = {"dp": dp + 1 - 2 * half}
     cap = own.shape[0] // 3
-    mid = cap // 2
     hid, width = w1_hbm.shape
     tokens = out_hbm.shape[0]
+    base, ext = slot_split(tokens)
+    eh = ext // 2
+    b_lo = fwd_up.shape[0] - eh
+    b_hi = base - b_lo
     counter = iter(range(N_COPIES))
 
     def rcopy(src, dst, dev):
@@ -141,20 +159,20 @@
         wx[1, m] = rcopy(w_in[m].at[hrow], w_all[m].at[wrow(1, core, half)], up)
         wx[3, m] = rcopy(w_in[m].at[hrow], w_all[m].at[wrow(3, core, half)], dn)
     split = hid * 9 // 38 // 16 * 16
-    common = hid - 2 * split
 
     def far(j, part):
-        if part == 0:
-            return pl.ds(pl.multiple_of((j * 2 + core) * hid, 16), common)
-        which = half if part == 1 else 1 - half
-        return pl.ds(pl.multiple_of((j * 2 + core) * hid + common + which * split, 16), split)
-
-    for part in (1, 0):
+        which = half if part in (0, 1) else 1 - half
+        start = (j * 2 + core) * hid + which * hh
+        if part in (1, 2):
+            return pl.ds(pl.multiple_of(start, 16), split)
+        return pl.ds(pl.multiple_of(start + split, 16), hh - split)
+
+    for part in (1, 0, 3):
         wx[2, 1, part] = rcopy(w1_all.at[far(1, part)], w1_all.at[far(2, part)], up)
         wx[2, 2, part] = rcopy(w2_all.at[far(3, part)], w2_all.at[far(2, part)], dn)
     for m in (1, 2):
         wy[2, m] = rcopy(w_all[m].at[far(2, 1)], w_all[m].at[far(2, 1)], pair)
-        for part in (0, 1, 2):
+        for part in range(4):
             wd[2, m, part] = rcopy(w_all[m].at[far(2, part)], w_all[m].at[far(2, part)], sib)
     for m in (1, 2):
         for j in (1, 3):
@@ -167,20 +185,29 @@
     d2d = {}
     for n, j in enumerate((2, 1, 3, 0)):
         d2d[j] = rcopy(for_sib.at[pl.ds((n % 2) * cap, cap)], sib_part.at[pl.ds(j * cap, cap)], sib)
+    def of(ref, block, at, size):
+        return ref.at[pl.ds(block * cap + at, size)]
+
     rows = {
-        "2u": rcopy(own.at[pl.ds(cap, mid)], fwd_up, up),
-        "2d": rcopy(own.at[pl.ds(cap + mid, mid)], fwd_dn, dn),
-        1: rcopy(own.at[pl.ds(0, cap)], got.at[pl.ds(cap, cap)], up),
-        3: rcopy(own.at[pl.ds(2 * cap, cap)], got.at[pl.ds(3 * cap, cap)], dn),
-        "fu": rcopy(fwd_up, got.at[pl.ds(2 * cap, mid)], up),
-        "fd": rcopy(fwd_dn, got.at[pl.ds(2 * cap + mid, mid)], dn),
+        "2ue": rcopy(of(own, 1, base, eh), fwd_up.at[pl.ds(b_lo, eh)], up),
+        "2de": rcopy(of(own, 1, base + eh, eh), fwd_dn.at[pl.ds(b_hi, eh)], dn),
+        "2ub": rcopy(of(own, 1, 0, b_lo), fwd_up.at[pl.ds(0, b_lo)], up),
+        "2db": rcopy(of(own, 1, b_lo, b_hi), fwd_dn.at[pl.ds(0, b_hi)], dn),
+        "1b": rcopy(of(own, 0, 0, base), of(got, 1, 0, base), up),
+        "1h": rcopy(of(own, 0, base + eh, eh), of(got, 1, base + eh, eh), up),
+        "1l": rcopy(of(own, 0, base, eh), of(got, 1, base, eh), up),
+        "3b": rcopy(of(own, 2, 0, base), of(got, 3, 0, base), dn),
+        "3l": rcopy(of(own, 2, base, eh), of(got, 3, base, eh), dn),
+        "3h": rcopy(of(own, 2, base + eh, eh), of(got, 3, base + eh, eh), dn),
+        "fu": rcopy(fwd_up.at[pl.ds(0, b_lo)], of(got, 2, 0, b_lo), up),
+        "fd": rcopy(fwd_dn.at[pl.ds(0, b_hi)], of(got, 2, b_lo, b_hi), dn),
     }
 
     for key in ((1, 1), (3, 1), (1, 2), (3, 2)):
         wx[key].start()
     wd[0, 1].start()
     wd[0, 2].start()
-    slot_tables(ids_ref, keys, slots_v, over_ref, chip, tp, chips, tiles * SUB, cap)
+    slot_tables(ids_ref, keys, slots_v, over_ref, chip, tp, chips, tiles * SUB, base)
     table[tiles] = jnp.zeros((SUB, width), jnp.bfloat16)
     lanes = slots_v.shape[1]
     fetch = [
@@ -195,10 +222,10 @@
         copy.wait()
 
     def pick_slots(j, c, dst, at):
-        base = (lax.rem(chip + j, chips) * 2 + c) * lanes
+        line = (lax.rem(chip + j, chips) * 2 + c) * lanes
 
         def body(i, carry):
-            dst[pl.ds(pl.multiple_of(at + i * 16, 16), 16), :] = pick_16(table, sidx, base + i * 16)
+            dst[pl.ds(pl.multiple_of(at + i * 16, 16), 16), :] = pick_16(table, sidx, line + i * 16)
             return carry
 
         lax.fori_loop(0, cap // 16, body, 0)
@@ -208,11 +235,19 @@
         ref, at = (got, 0) if j == 0 else (own, (j - 1) * cap)
 
         def body(i, carry):
-            a = pl.ds(pl.multiple_of(at + i * 32, 32), 32)
-            ref[a, :] = ref[a, :] + sib_part[pl.ds(pl.multiple_of(j * cap + i * 32, 32), 32), :]
+            a = pl.ds(pl.multiple_of(at + i * 16, 16), 16)
+            ref[a, :] = ref[a, :] + sib_part[pl.ds(pl.multiple_of(j * cap + i * 16, 16), 16), :]
             return carry
 
-        lax.fori_loop(0, cap // 32, body, 0)
+        lax.fori_loop(0, cap // 16, body, 0, unroll=3)
+
+    def add_far(at, far_ref, far_at):
+        def body(i, carry):
+            a = pl.ds(pl.multiple_of(at + i * 16, 16), 16)
+            own[a, :] = own[a, :] + far_ref[pl.ds(pl.multiple_of(far_at + i * 16, 16), 16), :]
+            return carry
+
+        lax.fori_loop(0, eh // 16, body, 0)
 
     def pick_sib(n, j):
         pick_slots(j, other, for_sib, (n % 2) * cap)
@@ -228,20 +263,22 @@
     pick_own(2)
     pick_sib(1, 1)
     add_part(2)
-    rows["2u"].start()
-    rows["2d"].start()
+    for key in ("2ue", "2de", "2ub", "2db"):
+        rows[key].start()
     pick_own(1)
     d2d[2].wait_send()
     pick_sib(2, 3)
     add_part(1)
-    rows[1].start()
+    rows["1b"].start()
+    rows["1h"].start()
     for j in (1, 3):
         wx[j, 1].wait_recv()
         wy[j, 1].start()
     pick_own(3)
     add_part(3)
-    rows[3].start()
-    for j in (1, 3):
+    rows["3b"].start()
+    rows["3l"].start()
+    for j in (3, 1):
         wx[j, 2].wait_recv()
         wy[j, 2].start()
     d2d[1].wait_send()
@@ -249,24 +286,24 @@
     pick_own(0)
     add_part(0)
 
-    slot = {0: 0, 1: 1, 3: 0, 2: 1}
+    slot = {0: 0, 3: 1, 1: 0, 2: 1}
     piece = 2 * hid
     load = {}
     for j in range(chips):
         for m in (1, 2):
-            base = (slot[j] * 2 + m - 1) * piece
+            w_at = (slot[j] * 2 + m - 1) * piece
             n = (j * 2 + m - 1) * 2
             if j == 0:
                 load[j, m] = [
-                    pltpu.make_async_copy(w_in[m], w_buf.at[pl.ds(pl.multiple_of(base + core * hid, 16), hid)],
+                    pltpu.make_async_copy(w_in[m], w_buf.at[pl.ds(pl.multiple_of(w_at + core * hid, 16), hid)],
                                           loc_sem.at[n]),
                     pltpu.make_async_copy(w_all[m].at[wrow(0, other)],
-                                          w_buf.at[pl.ds(pl.multiple_of(base + other * hid, 16), hid)],
+                                          w_buf.at[pl.ds(pl.multiple_of(w_at + other * hid, 16), hid)],
                                           loc_sem.at[n + 1]),
                 ]
             else:
                 load[j, m] = [
-                    pltpu.make_async_copy(w_all[m].at[pl.ds(j * piece, piece)], w_buf.at[pl.ds(base, piece)],
+                    pltpu.make_async_copy(w_all[m].at[pl.ds(j * piece, piece)], w_buf.at[pl.ds(w_at, piece)],
                                           loc_sem.at[n])
                 ]
 
@@ -278,20 +315,31 @@
     for m in (1, 2):
         wd[0, m].wait_recv()
     start_load(0)
-    rows["2u"].wait_recv()
+    rows["2ue"].wait_recv()
+    add_far(base, fwd_up, b_lo)
+    rows["1l"].start()
+    rows["2de"].wait_recv()
+    add_far(2 * cap + base + eh, fwd_dn, b_hi)
+    rows["3h"].start()
+    rows["2ub"].wait_recv()
     rows["fu"].start()
-    rows["2d"].wait_recv()
+    rows["2db"].wait_recv()
     rows["fd"].start()
+    for part in (1, 0):
+        for m in (1, 2):
+            wx[2, m, part].start()
     for j in (1, 3):
         for m in (1, 2):
             wd[j, m, 0].start()
-    for m in (1, 2):
-        for j in (1, 3):
-            wy[j, m].wait_recv()
-            wd[j, m, 1].start()
-            if (j, m) == (1, 1) or (j, m) == (3, 2):
-                wx[2, m, 1].start()
-                wx[2, m, 0].start()
+
+    def crossed(j, m):
+        wy[j, m].wait_recv()
+        wd[j, m, 1].start()
+        if (j, m) == (1, 1) or (j, m) == (3, 2):
+            wx[2, m, 3].start()
+
+    crossed(1, 1)
+    crossed(3, 1)
 
     gain = gain_ref[...].astype(jnp.float32)
     lines = tokens // 128
@@ -301,15 +349,28 @@
         def body(i, carry):
             at = pl.ds(pl.multiple_of(i * 512, 512), 512)
             total = None if start else y_ref[at, :]
+            def line_of(j):
+                line = lax.rem(chip + chips - j, chips) * ids_ref.shape[0] + tp * lines
+                return keys[pl.ds(pl.multiple_of(line, SUB), SUB), :].astype(jnp.float32)
+
+            anyone = line_of(0)
+            for j in range(1, chips):
+                anyone = jnp.maximum(anyone, line_of(j))
+            any_t = jnp.transpose(anyone)
+            lane = lax.broadcasted_iota(jnp.int32, any_t.shape, 1)
+
+            def column(key_t, r):
+                return jnp.sum(jnp.where(lane == 4 * i + r, key_t, 0.0), axis=1, keepdims=True)
+
             for j in sources:
-                line = lax.rem(chip + chips - j, chips) * ids_ref.shape[0] + tp * lines
-                key_t = jnp.transpose(keys[pl.ds(pl.multiple_of(line, SUB), SUB), :].astype(jnp.float32))
-                lane = lax.broadcasted_iota(jnp.int32, key_t.shape, 1)
+                size = base if j == 2 else cap
+                ids_of = slot_id[:, :size]
+                key_t = jnp.transpose(line_of(j))
                 hits = []
                 for r in range(4):
-                    col = jnp.sum(jnp.where(lane == 4 * i + r, key_t, 0.0), axis=1, keepdims=True)
-                    hits.append(jnp.where(col == slot_id, 1.0, 0.0).astype(jnp.bfloat16))
-                part = jnp.dot(jnp.concatenate(hits, axis=0), got[pl.ds(j * cap, cap), :],
+                    want = jnp.where(ids_of < base, column(key_t, r), column(any_t, r))
+                    hits.append(jnp.where(want == ids_of, 1.0, 0.0).astype(jnp.bfloat16))
+                part = jnp.dot(jnp.concatenate(hits, axis=0), got[pl.ds(j * cap, size), :],
                                preferred_element_type=jnp.float32)
                 total = part if total is None else total + part
             if not finish:
@@ -323,9 +384,10 @@
         lax.fori_loop(0, tokens // 512, body, 0)
 
     place((0,), True, False)
-    rows[1].wait_recv()
-    rows[3].wait_recv()
+    for key in ("1b", "3b", "1h", "3l", "1l", "3h"):
+        rows[key].wait_recv()
     place((1, 3), False, False)
+    crossed(3, 2)
     rows["fu"].wait_recv()
     rows["fd"].wait_recv()
     place((2,), False, True)
@@ -336,14 +398,14 @@
         for m in (1, 2):
             for copy in load[j, m]:
                 copy.wait()
-        base = slot[j] * 2 * piece
+        w_at = slot[j] * 2 * piece
 
         def body(i, carry):
             at = pl.ds(pl.multiple_of(i * block, block), block)
             n = sib_part[pl.ds(pl.multiple_of(tokens + i * block, block), block), :]
-            u = lax.dot_general(n, w_buf[pl.ds(base, piece), :], (((1,), (1,)), ((), ())),
+            u = lax.dot_general(n, w_buf[pl.ds(w_at, piece), :], (((1,), (1,)), ((), ())),
                                 preferred_element_type=jnp.float32)
-            y = jnp.dot(gelu(u), w_buf[pl.ds(base + piece, piece), :], preferred_element_type=jnp.float32)
+            y = jnp.dot(gelu(u), w_buf[pl.ds(w_at + piece, piece), :], preferred_element_type=jnp.float32)
             if not first:
                 y = y_ref[at, :] + y
             if last:
@@ -356,22 +418,26 @@
 
     def arrived(j):
         for m in (1, 2):
-            for k in (0, 1, 2) if j == 2 else (0, 1):
+            for k in range(4 if j == 2 else 2):
                 wd[j, m, k].wait_recv()
         start_load(j)
 
-    arrived(1)
+    arrived(3)
     mlp(0, first=True)
-    arrived(3)
-    mlp(1)
     for m in (1, 2):
         wx[2, m, 1].wait_recv()
         wy[2, m].start()
         wd[2, m, 1].start()
+    crossed(1, 2)
     mlp(3)
+    arrived(1)
     for m in (1, 2):
         wx[2, m, 0].wait_recv()
         wd[2, m, 0].start()
+    mlp(1)
+    for m in (1, 2):
+        wx[2, m, 3].wait_recv()
+        wd[2, m, 3].start()
     for m in (1, 2):
         wy[2, m].wait_recv()
         wd[2, m, 2].start()
@@ -412,7 +478,9 @@
         shard_rows, width = table.shape
         tokens = token_ids.shape[0] // ranks
         tp = lax.axis_index("tp")
-        cap = tokens * 17 // 32
+        base, ext = slot_split(tokens)
+        cap = base + ext
+        low = (base // 2 + 15) // 16 * 16
         hidden = w1.shape[1]
         bf, f32 = jnp.bfloat16, jnp.float32
         dma = pltpu.SemaphoreType.DMA
@@ -436,8 +504,8 @@
                 pltpu.VMEM((4 * cap, width), bf),
                 pltpu.VMEM((2 * cap, width), bf),
                 pltpu.VMEM((4 * cap, width), bf),
-                pltpu.VMEM((cap // 2, width), bf),
-                pltpu.VMEM((cap // 2, width), bf),
+                pltpu.VMEM((low + ext // 2, width), bf),
+                pltpu.VMEM((base - low + ext // 2, width), bf),
                 pltpu.VMEM((tokens, width), f32),
                 pltpu.VMEM((8 * hidden, width), bf),
                 pltpu.VMEM((chips * lines, 128), jnp.int32),

time: 125 us -> 111 us (0.89)
  Pallas kernels: 119 us -> 105 us
    pallas_call x1, Pallas kernels: 116 us -> 103 us  [device_step(): pl.pallas_call(functools.partial(block_kernel, chips), out_shape=[jax.Sha...]
where the time goes in v1:
time: 111 us; the launch traced here: 109 us
  Pallas kernels  105 us (95%)
  local copies, waits for them, and re-layouts  3.68 us (3%)
    pallas_call x1, Pallas kernels, device_step(): pl.pallas_call(functools.partial(block_kernel, chips), out_shape=[jax.Sha...  103 us
    pallas_call x1, Pallas kernels, settle(): pl.pallas_call(copy_kernel, out_shape=jax.ShapeDtypeStruct(res.shape, res...  2.31 us

profile of v1, /device:TPU:112, one launch (start us, length us, event | category | flops | bytes accessed | tf_op | source)
XLA Modules:
  0.0 109.5 jit_solution(7284350126630466302)
XLA Ops:
  0.0 1.3 %reshape.32.gain_ref = bf16[1,896]{1,0:T(2,128)(2,1)} reshape(bf16[896]{0:T(1024)(128)(2,1)} %param.9) | data formatting | bytes 3584 | tf_op jit(solution)/shard_map/reshape | solution.py:520
  1.3 102.8 %shard_map.57 = (bf16[1024,896]{1,0:T(8,128)(2,1)}, f32[8,128]{1,0:T(8,128)}, bf16[4864,896]{1,0:T(8,128)(2,1)}, bf16[4864,896]{1,0:T(8,128)(2,1)}) custom-call(s32[64,128]{1,0:T(8,128)} %bitcast.12, bf16[2374,8,896]{2,1,0:T(8,128)(2,1)} %bitcast.8, bf16[1,896]{1,0:T(2,128)(2,1)} %reshape.32.gain_ref, bf16[608,896]{1,0:T(8,128)(2,1)} %bitcast.11, ...), custom_call_target="tpu_custom_call" | custom-call | tf_op jit(solution)/shard_map/pallas_call | solution.py:491
  104.0 1.2 %slice.3 = f32[1,1]{1,0:T(1,128)} slice(f32[8,128]{1,0:T(8,128)} %get-tuple-element.37), slice={[0:1], [0:1]} | slice | bytes 8 | tf_op jit(solution)/shard_map/slice | solution.py:521
  105.9 2.3 %conditional.1 = (bf16[1024,896]{1,0:T(8,128)(2,1)S(1)}) conditional(s32[]{:T(128)} %bitcast.5, bf16[1024,896]{1,0:T(8,128)(2,1)} %get-tuple-element.38, (s32[]{:T(128)}, s32[8192]{0:T(1024)}, bf16[18992,896]{1,0:T(8,128)(2,1)}, bf16[896]{0:T(1024)(128)(2,1)}, bf16[896,608]{0,1:T(8,128)(2,1)}, /*index=5*/bf16[4864,896]{1,0:T(8,128)(2,1)}, ...), branch_computations={%region_0.0_spmd, %region_1.4_spmd} | conditional | flops 17933330432 | bytes 195280992 | solution.py:537
  105.9 2.3 %branch_0_fun.1 = bf16[1024,896]{1,0:T(8,128)(2,1)S(1)} custom-call(bf16[1024,896]{1,0:T(8,128)(2,1)} %src), custom_call_target="tpu_custom_call" | custom-call | tf_op jit(solution)/shard_map/cond/branch_0_fun/pallas_call | solution.py:464
  108.2 0.0 copy-start.3
  108.2 1.2 %copy-done.3 = bf16[1024,896]{1,0:T(8,128)(2,1)} copy-done((bf16[1024,896]{1,0:T(8,128)(2,1)}, bf16[1024,896]{1,0:T(8,128)(2,1)S(1)}, u32[]{:S(2)}) %copy-start.3) | copy-done | bytes 1835032
Async XLA Ops:
  108.2 1.2 %copy-start.3 = (bf16[1024,896]{1,0:T(8,128)(2,1)}, bf16[1024,896]{1,0:T(8,128)(2,1)S(1)}, u32[]{:S(2)}) copy-start(bf16[1024,896]{1,0:T(8,128)(2,1)S(1)} %get-tuple-element.54) | copy-start | bytes 5505028
